TPU v7x, 32 devices: a whole 2x2x4 slice. The times are simulated.
32 devices in a mesh: dp: 2 (over x), ep: 16 (over z, y, core).
Axes of the slice: x: 2, y: 2, z: 4, core: 2. Of those that a mesh axis runs over, the one named last changes fastest.
Arguments:
- tokens: bfloat16 [256, 3584], P(('dp', 'ep')), may hold values from -6 to 6
- expert_ids: int32 [2, 256, 8], P(None, ('dp', 'ep')), may hold values from 0 to 15, all different within a row; in each aligned block of 8 rows (0 to 7, 8 to 15, ..., all dimensions but the last counted through in order) at most 6 rows name the same one
- quant_gates: int32 [2, 256, 8], P(None, ('dp', 'ep')), may hold values from 1 to 63
- w_gate: bfloat16 [2, 16, 3584, 1024], P(None, 'ep', None, 'dp'), may hold values from -0.09375 to 0.09375
- w_up: bfloat16 [2, 16, 3584, 1024], P(None, 'ep', None, 'dp'), may hold values from -0.09375 to 0.09375
- w_down: bfloat16 [2, 16, 1024, 3584], P(None, 'ep', 'dp'), may hold values from -0.1875 to 0.1875
Outputs:
- stream_out: bfloat16 [256, 3584], P(('dp', 'ep'))
- expert_load: int32 [2, 16], replicated
Inputs may be any that keep to these rules, and one draw needn't show every extreme that they name: `expert_ids`: in each layer, the 8 tokens of one device name any one expert at most 6 times, a bound that some block reaches.
All inputs are finite; a program needn't handle non-finite values.
Results may differ from a plain program's by a relative error of at most 0.015.
Values may be sent and summed in bfloat16 or wider, within the bound.
A program may use at most 64 MiB of HBM per device.

v0:
```python
import jax
import jax.numpy as jnp
from jax import lax
from jax.sharding import PartitionSpec as P

ROUTE_SCALE = 2.827
EPS = 1e-06


def slot_tables(ids, quant, experts, capacity):
    count_tok, top = ids.shape
    flat = ids.reshape(count_tok * top)
    expert_iota = lax.broadcasted_iota(jnp.int32, (count_tok * top, experts), 1)
    onehot = (flat[:, None] == expert_iota).astype(jnp.int32)
    earlier = jnp.cumsum(onehot, axis=0) - onehot
    position = jnp.sum(earlier * onehot, axis=1)
    target = flat * capacity + position
    slot_iota = lax.broadcasted_iota(jnp.int32, (count_tok * top, experts * capacity), 1)
    picked = target[:, None] == slot_iota
    quant_wide = quant.astype(jnp.float32)
    gates = (ROUTE_SCALE * quant_wide / jnp.sum(quant_wide, axis=1, keepdims=True)).reshape(
        count_tok * top
    )
    spread = jnp.sum(
        jnp.where(picked, gates[:, None], 0.0).reshape(count_tok, top, experts * capacity), axis=1
    )
    chosen = jnp.sum(picked.astype(jnp.float32).reshape(count_tok, top, experts * capacity), axis=1)
    counts = jnp.sum(onehot, axis=0)
    return (chosen, spread, counts)


def per_device(tokens, expert_ids, quant_gates, w_gate, w_up, w_down):
    layers, count_tok, top = expert_ids.shape
    n_ep = lax.axis_size("ep")
    capacity = min(count_tok, max(2, 3 * count_tok * top // (2 * n_ep)))
    width = tokens.shape[1]
    state = tokens
    table = jnp.stack(
        [
            slot_tables(expert_ids[layer], quant_gates[layer], n_ep, capacity)[2]
            for layer in range(layers)
        ]
    )
    loads = lax.psum(table, ("dp", "ep"))
    for layer in range(layers):
        chosen, spread, counts = slot_tables(expert_ids[layer], quant_gates[layer], n_ep, capacity)
        wide = state.astype(jnp.float32)
        normed = (wide * lax.rsqrt(jnp.mean(wide * wide, axis=1, keepdims=True) + EPS)).astype(
            jnp.bfloat16
        )
        outgoing = jnp.dot(
            chosen.T.astype(jnp.bfloat16), normed, preferred_element_type=jnp.float32
        ).astype(jnp.bfloat16)
        arrived = lax.all_to_all(
            outgoing.reshape(n_ep, capacity, width), "ep", split_axis=0, concat_axis=0, tiled=True
        )
        arrived = arrived.reshape(n_ep * capacity, width)
        weight_gate = w_gate[layer, 0]
        weight_up = w_up[layer, 0]
        weight_down = w_down[layer, 0]
        piece = lax.all_gather(arrived, "dp", axis=0, tiled=True)
        gate = jnp.dot(piece, weight_gate, preferred_element_type=jnp.float32)
        upper = jnp.dot(piece, weight_up, preferred_element_type=jnp.float32)
        hidden = (jax.nn.silu(gate) * upper).astype(jnp.bfloat16)
        partial_out = jnp.dot(hidden, weight_down, preferred_element_type=jnp.float32)
        parts = partial_out.astype(jnp.bfloat16)
        summed = lax.psum_scatter(
            parts.astype(jnp.float32).astype(jnp.bfloat16), "dp", scatter_dimension=0, tiled=True
        ).astype(jnp.float32)
        returned = lax.all_to_all(
            summed.reshape(n_ep, capacity, width).astype(jnp.bfloat16),
            "ep",
            split_axis=0,
            concat_axis=0,
            tiled=True,
        ).astype(jnp.float32)
        branch = jnp.dot(
            spread,
            returned.reshape(n_ep * capacity, width),
            precision=lax.Precision.HIGHEST,
            preferred_element_type=jnp.float32,
        )
        state = (state.astype(jnp.float32) + branch).astype(jnp.bfloat16)
    return (state, loads)


def solution(mesh):
    return jax.shard_map(
        per_device,
        mesh=mesh,
        in_specs=(
            P(("dp", "ep"), None),
            P(None, ("dp", "ep"), None),
            P(None, ("dp", "ep"), None),
            P(None, "ep", None, "dp"),
            P(None, "ep", None, "dp"),
            P(None, "ep", "dp", None),
        ),
        out_specs=(P(("dp", "ep"), None), P()),
        check_vma=False,
    )
```

profile of v0, /device:TPU:0, one launch (start us, length us, event | category | flops | bytes accessed | tf_op | source)
XLA Modules:
  0.0 278.6 jit_solution(12670127936095068034)
XLA Ops:
  7.2 1.0 fusion.47
  8.2 0.9 convert_reduce_fusion.2
  9.0 0.7 fusion.60
  10.1 0.2 fusion.54
  10.8 0.8 bitcast_divide_fusion
  11.6 0.7 bitcast_add_fusion
  12.4 1.2 convolution_convert_fusion.3
  13.6 0.2 reshape.136
  13.9 29.6 %all_to_all.20 = bf16[16,6,3584]{2,1,0:T(8,128)(2,1)S(1)} all-to-all(bf16[16,6,3584]{2,1,0:T(8,128)(2,1)S(1)} %reshape.136), channel_id=1, replica_groups=mesh['dp'=2,'ep'=16] {'ep'}, dimensions={0} | all-to-all | bytes 1376256 | tf_op jit(solution)/shard_map/all_to_all | solution.py:54
  43.5 1.1 reshape.137
  44.7 24.9 %all-gather.3.cloned.1.call-done = bf16[192,3584]{1,0:T(8,128)(2,1)} async-done(((bf16[96,3584]{1,0:T(8,128)(2,1)}), bf16[192,3584]{1,0:T(8,128)(2,1)}) %all-gather.3.cloned.1.call-update) | async-done | bytes 1376272 | tf_op jit(solution)/shard_map/all_gather | solution.py:61
  69.6 3.4 %fusion.11 = f32[192,512]{1,0:T(8,128)S(1)} fusion(bf16[192,3584]{1,0:T(8,128)(2,1)} %all-gather.3.cloned.1.call-done, bf16[2,1,3584,512]{3,2,1,0:T(8,128)(2,1)} %param.9), kind=kOutput, calls=%fused_computation.17 | convolution fusion | flops 704643072 | bytes 5439488 | tf_op jit(solution)/shard_map/dot_general | solution.py:62
  73.0 5.9 %convolution_convert_fusion.1 = bf16[192,3584]{1,0:T(8,128)(2,1)} fusion(bf16[2,1,512,3584]{3,2,1,0:T(8,128)(2,1)} %param.11, bf16[192,3584]{1,0:T(8,128)(2,1)S(1)} %copy-done.1, bf16[2,1,3584,512]{3,2,1,0:T(8,128)(2,1)} %param.10, f32[192,512]{1,0:T(8,128)S(1)} %fusion.11), kind=kOutput, calls=%fused_computation.1 | convolution fusion | flops 1410564096 | bytes 10485760 | tf_op jit(solution)/shard_map/dot_general | solution.py:65
  79.0 24.1 %reduce-scatter.3.cloned.1.call-done = bf16[96,3584]{1,0:T(8,128)(2,1)} async-done(((bf16[192,3584]{1,0:T(8,128)(2,1)}), bf16[96,3584]{1,0:T(8,128)(2,1)}) %reduce-scatter.3.cloned.1.call-update) | async-done | bytes 688144 | tf_op jit(solution)/shard_map/reduce_scatter | solution.py:67
  103.2 2.1 convert_element_type.103
  105.3 5.6 %all-to-all-start.1 = ((bf16[16,6,3584]{2,1,0:T(8,128)(2,1)}), bf16[16,6,3584]{2,1,0:T(8,128)(2,1)S(1)}, u32[]{:S(2)}, u32[]{:S(2)}) async-start(bf16[16,6,3584]{2,1,0:T(8,128)(2,1)} %convert_element_type.103), calls=%async_computation.2 | async-start | bytes 1835008 | tf_op jit(solution)/shard_map/all_to_all | solution.py:70
  111.1 20.6 %all-to-all-done.1 = bf16[16,6,3584]{2,1,0:T(8,128)(2,1)S(1)} async-done(((bf16[16,6,3584]{2,1,0:T(8,128)(2,1)}), bf16[16,6,3584]{2,1,0:T(8,128)(2,1)S(1)}, u32[]{:S(2)}, u32[]{:S(2)}) %all-to-all-start.1) | async-done | bytes 688160 | tf_op jit(solution)/shard_map/all_to_all | solution.py:70
  131.7 0.2 reshape.138
  132.0 0.5 multiply_reduce_fusion
  132.5 0.4 convolution_convert_fusion.2
  132.9 0.2 reshape.139
  133.1 28.3 %all_to_all.21 = bf16[16,6,3584]{2,1,0:T(8,128)(2,1)S(1)} all-to-all(bf16[16,6,3584]{2,1,0:T(8,128)(2,1)S(1)} %reshape.139), channel_id=1, replica_groups=mesh['dp'=2,'ep'=16] {'ep'}, dimensions={0} | all-to-all | bytes 1376256 | tf_op jit(solution)/shard_map/all_to_all | solution.py:54
  161.4 1.1 reshape.140
  162.6 24.0 %all-gather.5.cloned.1.call-done = bf16[192,3584]{1,0:T(8,128)(2,1)} async-done(((bf16[96,3584]{1,0:T(8,128)(2,1)}), bf16[192,3584]{1,0:T(8,128)(2,1)}) %all-gather.5.cloned.1.call-update) | async-done | bytes 1376272 | tf_op jit(solution)/shard_map/all_gather | solution.py:61
  186.6 3.4 %fusion.6 = f32[192,512]{1,0:T(8,128)S(1)} fusion(bf16[192,3584]{1,0:T(8,128)(2,1)} %all-gather.5.cloned.1.call-done, bf16[2,1,3584,512]{3,2,1,0:T(8,128)(2,1)} %param.9), kind=kOutput, calls=%fused_computation.12 | convolution fusion | flops 704643072 | bytes 5439488 | tf_op jit(solution)/shard_map/dot_general | solution.py:62
  190.0 5.9 %convolution_convert_fusion = bf16[192,3584]{1,0:T(8,128)(2,1)} fusion(bf16[2,1,512,3584]{3,2,1,0:T(8,128)(2,1)} %param.11, bf16[192,3584]{1,0:T(8,128)(2,1)S(1)} %copy-done.2, bf16[2,1,3584,512]{3,2,1,0:T(8,128)(2,1)} %param.10, f32[192,512]{1,0:T(8,128)S(1)} %fusion.6), kind=kOutput, calls=%fused_computation | convolution fusion | flops 1410564096 | bytes 10485760 | tf_op jit(solution)/shard_map/dot_general | solution.py:65
  196.0 24.1 %reduce-scatter.5.cloned.1.call-done = bf16[96,3584]{1,0:T(8,128)(2,1)} async-done(((bf16[192,3584]{1,0:T(8,128)(2,1)}), bf16[96,3584]{1,0:T(8,128)(2,1)}) %reduce-scatter.5.cloned.1.call-update) | async-done | bytes 688144 | tf_op jit(solution)/shard_map/reduce_scatter | solution.py:67
  220.1 2.1 convert_element_type.114
  222.3 5.6 %all-to-all-start.3 = ((bf16[16,6,3584]{2,1,0:T(8,128)(2,1)}), bf16[16,6,3584]{2,1,0:T(8,128)(2,1)S(1)}, u32[]{:S(2)}, u32[]{:S(2)}) async-start(bf16[16,6,3584]{2,1,0:T(8,128)(2,1)} %convert_element_type.114), calls=%async_computation.5 | async-start | bytes 1835008 | tf_op jit(solution)/shard_map/all_to_all | solution.py:70
  227.9 42.9 %psum.7 = s32[2,16]{1,0:T(2,128)} all-reduce(s32[2,16]{1,0:T(2,128)S(1)} %pad_add_fusion), channel_id=1, replica_groups=mesh['dp'=2,'ep'=16] {'dp','ep'}, use_global_device_ids=true, to_apply=%region_16.17 | all-reduce | flops 32 | bytes 256 | tf_op jit(solution)/shard_map/psum | solution.py:44
  270.9 0.2 reshape.141
  271.1 1.0 fusion.2
  (29 shorter events, 1.3 us)
Async XLA Ops:
  7.2 62.4 %all-gather.3.cloned.1.call-start = ((), (), s32[]{:S(2)}) async-start(), calls=%async_computation.6 | async-start | bytes 2064384 | tf_op jit(solution)/shard_map/all_gather | solution.py:61
  44.6 58.5 %reduce-scatter.3.cloned.1.call-start = ((), (), s32[]{:S(2)}) async-start(), calls=%async_computation.7 | async-start | bytes 2064384 | tf_op jit(solution)/shard_map/reduce_scatter | solution.py:67
  69.6 3.4 %copy-start.1 = (bf16[192,3584]{1,0:T(8,128)(2,1)S(1)}, bf16[192,3584]{1,0:T(8,128)(2,1)}, u32[]{:S(2)}) copy-start(bf16[192,3584]{1,0:T(8,128)(2,1)} %all-gather.3.cloned.1.call-done) | copy-start | bytes 4128772
  79.0 53.0 %copy-start = (bf16[8,3584]{1,0:T(8,128)(2,1)S(1)}, bf16[8,3584]{1,0:T(8,128)(2,1)}, u32[]{:S(2)}) copy-start(bf16[8,3584]{1,0:T(8,128)(2,1)} %param.6) | copy-start | bytes 172036
  105.3 26.4 %all-to-all-start.1 = ((bf16[16,6,3584]{2,1,0:T(8,128)(2,1)}), bf16[16,6,3584]{2,1,0:T(8,128)(2,1)S(1)}, u32[]{:S(2)}, u32[]{:S(2)}) async-start(bf16[16,6,3584]{2,1,0:T(8,128)(2,1)} %convert_element_type.103), calls=%async_computation.2 | async-start | bytes 1835008 | tf_op jit(solution)/shard_map/all_to_all | solution.py:70
  110.9 75.7 %all-gather.5.cloned.1.call-start = ((), (), s32[]{:S(2)}) async-start(), calls=%async_computation.8 | async-start | bytes 2064384 | tf_op jit(solution)/shard_map/all_gather | solution.py:61
  162.5 57.6 %reduce-scatter.5.cloned.1.call-start = ((), (), s32[]{:S(2)}) async-start(), calls=%async_computation.9 | async-start | bytes 2064384 | tf_op jit(solution)/shard_map/reduce_scatter | solution.py:67
  186.6 3.4 %copy-start.2 = (bf16[192,3584]{1,0:T(8,128)(2,1)S(1)}, bf16[192,3584]{1,0:T(8,128)(2,1)}, u32[]{:S(2)}) copy-start(bf16[192,3584]{1,0:T(8,128)(2,1)} %all-gather.5.cloned.1.call-done) | copy-start | bytes 4128772
  222.3 48.6 %all-to-all-start.3 = ((bf16[16,6,3584]{2,1,0:T(8,128)(2,1)}), bf16[16,6,3584]{2,1,0:T(8,128)(2,1)S(1)}, u32[]{:S(2)}, u32[]{:S(2)}) async-start(bf16[16,6,3584]{2,1,0:T(8,128)(2,1)} %convert_element_type.114), calls=%async_computation.5 | async-start | bytes 1835008 | tf_op jit(solution)/shard_map/all_to_all | solution.py:70
Sparse Core Ops, SparseCore 0:
  44.7 24.8 all-gather.2
  79.1 23.9 reduce-scatter.2
  162.7 23.8 all-gather.4
  196.1 23.9 reduce-scatter.4
where the time goes:
time: 279 us
  waiting for transfers between devices  118 us (42%)
  blocking collectives  101 us (36%)
  matrix products  21.8 us (8%)
  between operations  13.9 us (5%)
  starting transfers between devices  11.4 us (4%)
  local copies, waits for them, and re-layouts  8.5 us (3%)
  other arithmetic  4.25 us (2%)
    all_to_all x2, blocking collectives, per_device(): lax.all_to_all(outgoing.reshape(n_ep, capacity, width), 'ep', split_axis=...  57.9 us
    all_gather x2, waiting for transfers between devices, per_device(): piece = lax.all_gather(arrived, 'dp', axis=0, tiled=True)  48.9 us
    reduce_scatter x2, waiting for transfers between devices, per_device(): lax.psum_scatter(parts.astype(jnp.float32).astype(jnp.bfloat16), 'dp', sc...  48.3 us
    psum x1, blocking collectives, per_device(): loads = lax.psum(table, ('dp', 'ep'))  42.9 us
    all_to_all x2, waiting for transfers between devices, per_device(): lax.all_to_all(summed.reshape(n_ep, capacity, width).astype(jnp.bfloat16)...  20.6 us
    dot_general x2, matrix products, per_device(): jnp.dot(hidden, weight_down, preferred_element_type=jnp.float32)  11.9 us
    all_to_all x2, starting transfers between devices, per_device(): lax.all_to_all(summed.reshape(n_ep, capacity, width).astype(jnp.bfloat16)...  11.2 us
    dot_general x2, matrix products, per_device(): gate = jnp.dot(piece, weight_gate, preferred_element_type=jnp.float32)  6.86 us
  transfers between devices with their start and end apart: 6, of which 5 were waited for; matrix products, arithmetic and copies ran while one was open for 0% of the time, Pallas kernels for 0%

commit v1 on v0

--- a/solution.py
+++ b/solution.py
@@ -41,7 +41,7 @@
             for layer in range(layers)
         ]
     )
-    loads = lax.psum(table, ("dp", "ep"))
+    loads = lax.psum(lax.psum(table, "ep"), "dp")
     for layer in range(layers):
         chosen, spread, counts = slot_tables(expert_ids[layer], quant_gates[layer], n_ep, capacity)
         wide = state.astype(jnp.float32)

time: 279 us -> 265 us (0.950)
  blocking collectives: 101 us -> 86.6 us
    psum x1 -> x2, blocking collectives: 42.9 us -> 28.7 us  [per_device(): loads = lax.psum(lax.psum(table, 'ep'), 'dp')]
where the time goes in v1:
time: 265 us; the launch traced here: 264 us
  waiting for transfers between devices  118 us (45%)
  blocking collectives  86.6 us (33%)
  matrix products  21.8 us (8%)
  between operations  13.9 us (5%)
  starting transfers between devices  11.4 us (4%)
  local copies, waits for them, and re-layouts  8.5 us (3%)
  other arithmetic  4.25 us (2%)
    all_to_all x2, blocking collectives, per_device(): lax.all_to_all(outgoing.reshape(n_ep, capacity, width), 'ep', split_axis=...  57.9 us
    all_gather x2, waiting for transfers between devices, per_device(): piece = lax.all_gather(arrived, 'dp', axis=0, tiled=True)  48.9 us
    reduce_scatter x2, waiting for transfers between devices, per_device(): lax.psum_scatter(parts.astype(jnp.float32).astype(jnp.bfloat16), 'dp', sc...  48.3 us
    psum x2, blocking collectives, per_device(): loads = lax.psum(lax.psum(table, 'ep'), 'dp')  28.7 us
    all_to_all x2, waiting for transfers between devices, per_device(): lax.all_to_all(summed.reshape(n_ep, capacity, width).astype(jnp.bfloat16)...  20.6 us
    dot_general x2, matrix products, per_device(): jnp.dot(hidden, weight_down, preferred_element_type=jnp.float32)  11.9 us
    all_to_all x2, starting transfers between devices, per_device(): lax.all_to_all(summed.reshape(n_ep, capacity, width).astype(jnp.bfloat16)...  11.2 us
    dot_general x2, matrix products, per_device(): gate = jnp.dot(piece, weight_gate, preferred_element_type=jnp.float32)  6.86 us
  transfers between devices with their start and end apart: 6, of which 5 were waited for; matrix products, arithmetic and copies ran while one was open for 0% of the time, Pallas kernels for 0%

profile of v1, /device:TPU:0, one launch (start us, length us, event | category | flops | bytes accessed | tf_op | source)
XLA Modules:
  0.0 264.4 jit_solution(4663025497791743629)
XLA Ops:
  7.2 1.0 fusion.47
  8.2 0.9 convert_reduce_fusion.2
  9.0 0.7 fusion.60
  10.8 0.8 bitcast_divide_fusion
  11.6 0.7 bitcast_add_fusion
  12.4 1.2 convolution_convert_fusion.3
  13.6 0.2 reshape.136
  13.9 29.6 %all_to_all.20 = bf16[16,6,3584]{2,1,0:T(8,128)(2,1)S(1)} all-to-all(bf16[16,6,3584]{2,1,0:T(8,128)(2,1)S(1)} %reshape.136), channel_id=1, replica_groups=mesh['dp'=2,'ep'=16] {'ep'}, dimensions={0} | all-to-all | bytes 1376256 | tf_op jit(solution)/shard_map/all_to_all | solution.py:54
  43.5 1.1 reshape.137
  44.7 24.9 %all-gather.3.cloned.1.call-done = bf16[192,3584]{1,0:T(8,128)(2,1)} async-done(((bf16[96,3584]{1,0:T(8,128)(2,1)}), bf16[192,3584]{1,0:T(8,128)(2,1)}) %all-gather.3.cloned.1.call-update) | async-done | bytes 1376272 | tf_op jit(solution)/shard_map/all_gather | solution.py:61
  69.6 3.4 %fusion.11 = f32[192,512]{1,0:T(8,128)S(1)} fusion(bf16[192,3584]{1,0:T(8,128)(2,1)} %all-gather.3.cloned.1.call-done, bf16[2,1,3584,512]{3,2,1,0:T(8,128)(2,1)} %param.9), kind=kOutput, calls=%fused_computation.17 | convolution fusion | flops 704643072 | bytes 5439488 | tf_op jit(solution)/shard_map/dot_general | solution.py:62
  73.0 5.9 %convolution_convert_fusion.1 = bf16[192,3584]{1,0:T(8,128)(2,1)} fusion(bf16[2,1,512,3584]{3,2,1,0:T(8,128)(2,1)} %param.11, bf16[192,3584]{1,0:T(8,128)(2,1)S(1)} %copy-done.1, bf16[2,1,3584,512]{3,2,1,0:T(8,128)(2,1)} %param.10, f32[192,512]{1,0:T(8,128)S(1)} %fusion.11), kind=kOutput, calls=%fused_computation.1 | convolution fusion | flops 1410564096 | bytes 10485760 | tf_op jit(solution)/shard_map/dot_general | solution.py:65
  79.0 24.1 %reduce-scatter.3.cloned.1.call-done = bf16[96,3584]{1,0:T(8,128)(2,1)} async-done(((bf16[192,3584]{1,0:T(8,128)(2,1)}), bf16[96,3584]{1,0:T(8,128)(2,1)}) %reduce-scatter.3.cloned.1.call-update) | async-done | bytes 688144 | tf_op jit(solution)/shard_map/reduce_scatter | solution.py:67
  103.2 2.1 convert_element_type.103
  105.3 5.6 %all-to-all-start.1 = ((bf16[16,6,3584]{2,1,0:T(8,128)(2,1)}), bf16[16,6,3584]{2,1,0:T(8,128)(2,1)S(1)}, u32[]{:S(2)}, u32[]{:S(2)}) async-start(bf16[16,6,3584]{2,1,0:T(8,128)(2,1)} %convert_element_type.103), calls=%async_computation.2 | async-start | bytes 1835008 | tf_op jit(solution)/shard_map/all_to_all | solution.py:70
  111.1 20.6 %all-to-all-done.1 = bf16[16,6,3584]{2,1,0:T(8,128)(2,1)S(1)} async-done(((bf16[16,6,3584]{2,1,0:T(8,128)(2,1)}), bf16[16,6,3584]{2,1,0:T(8,128)(2,1)S(1)}, u32[]{:S(2)}, u32[]{:S(2)}) %all-to-all-start.1) | async-done | bytes 688160 | tf_op jit(solution)/shard_map/all_to_all | solution.py:70
  131.7 0.2 reshape.138
  132.0 0.5 multiply_reduce_fusion
  132.5 0.4 convolution_convert_fusion.2
  132.9 0.2 reshape.139
  133.1 28.3 %all_to_all.21 = bf16[16,6,3584]{2,1,0:T(8,128)(2,1)S(1)} all-to-all(bf16[16,6,3584]{2,1,0:T(8,128)(2,1)S(1)} %reshape.139), channel_id=1, replica_groups=mesh['dp'=2,'ep'=16] {'ep'}, dimensions={0} | all-to-all | bytes 1376256 | tf_op jit(solution)/shard_map/all_to_all | solution.py:54
  161.4 1.1 reshape.140
  162.6 24.0 %all-gather.5.cloned.1.call-done = bf16[192,3584]{1,0:T(8,128)(2,1)} async-done(((bf16[96,3584]{1,0:T(8,128)(2,1)}), bf16[192,3584]{1,0:T(8,128)(2,1)}) %all-gather.5.cloned.1.call-update) | async-done | bytes 1376272 | tf_op jit(solution)/shard_map/all_gather | solution.py:61
  186.6 3.4 %fusion.6 = f32[192,512]{1,0:T(8,128)S(1)} fusion(bf16[192,3584]{1,0:T(8,128)(2,1)} %all-gather.5.cloned.1.call-done, bf16[2,1,3584,512]{3,2,1,0:T(8,128)(2,1)} %param.9), kind=kOutput, calls=%fused_computation.12 | convolution fusion | flops 704643072 | bytes 5439488 | tf_op jit(solution)/shard_map/dot_general | solution.py:62
  190.0 5.9 %convolution_convert_fusion = bf16[192,3584]{1,0:T(8,128)(2,1)} fusion(bf16[2,1,512,3584]{3,2,1,0:T(8,128)(2,1)} %param.11, bf16[192,3584]{1,0:T(8,128)(2,1)S(1)} %copy-done.2, bf16[2,1,3584,512]{3,2,1,0:T(8,128)(2,1)} %param.10, f32[192,512]{1,0:T(8,128)S(1)} %fusion.6), kind=kOutput, calls=%fused_computation | convolution fusion | flops 1410564096 | bytes 10485760 | tf_op jit(solution)/shard_map/dot_general | solution.py:65
  196.0 24.1 %reduce-scatter.5.cloned.1.call-done = bf16[96,3584]{1,0:T(8,128)(2,1)} async-done(((bf16[192,3584]{1,0:T(8,128)(2,1)}), bf16[96,3584]{1,0:T(8,128)(2,1)}) %reduce-scatter.5.cloned.1.call-update) | async-done | bytes 688144 | tf_op jit(solution)/shard_map/reduce_scatter | solution.py:67
  220.1 2.1 convert_element_type.114
  222.3 5.6 %all-to-all-start.3 = ((bf16[16,6,3584]{2,1,0:T(8,128)(2,1)}), bf16[16,6,3584]{2,1,0:T(8,128)(2,1)S(1)}, u32[]{:S(2)}, u32[]{:S(2)}) async-start(bf16[16,6,3584]{2,1,0:T(8,128)(2,1)} %convert_element_type.114), calls=%async_computation.5 | async-start | bytes 1835008 | tf_op jit(solution)/shard_map/all_to_all | solution.py:70
  227.9 23.9 %psum.14 = s32[2,16]{1,0:T(2,128)S(1)} all-reduce(s32[2,16]{1,0:T(2,128)S(1)} %pad_add_fusion), channel_id=1, replica_groups=mesh['dp'=2,'ep'=16] {'ep'}, use_global_device_ids=true, to_apply=%region_16.17 | all-reduce | flops 32 | bytes 256 | tf_op jit(solution)/shard_map/psum | solution.py:44
  251.8 4.8 %psum.15 = s32[2,16]{1,0:T(2,128)} all-reduce(s32[2,16]{1,0:T(2,128)S(1)} %psum.14), channel_id=1, replica_groups=mesh['dp'=2,'ep'=16] {'dp'}, use_global_device_ids=true, to_apply=%region_17.18 | all-reduce | flops 32 | bytes 256 | tf_op jit(solution)/shard_map/psum | solution.py:44
  256.6 0.2 reshape.141
  256.8 1.0 fusion.2
  (30 shorter events, 1.5 us)
Async XLA Ops:
  7.2 62.4 %all-gather.3.cloned.1.call-start = ((), (), s32[]{:S(2)}) async-start(), calls=%async_computation.6 | async-start | bytes 2064384 | tf_op jit(solution)/shard_map/all_gather | solution.py:61
  44.6 58.5 %reduce-scatter.3.cloned.1.call-start = ((), (), s32[]{:S(2)}) async-start(), calls=%async_computation.7 | async-start | bytes 2064384 | tf_op jit(solution)/shard_map/reduce_scatter | solution.py:67
  69.6 3.4 %copy-start.1 = (bf16[192,3584]{1,0:T(8,128)(2,1)S(1)}, bf16[192,3584]{1,0:T(8,128)(2,1)}, u32[]{:S(2)}) copy-start(bf16[192,3584]{1,0:T(8,128)(2,1)} %all-gather.3.cloned.1.call-done) | copy-start | bytes 4128772
  79.0 53.0 %copy-start = (bf16[8,3584]{1,0:T(8,128)(2,1)S(1)}, bf16[8,3584]{1,0:T(8,128)(2,1)}, u32[]{:S(2)}) copy-start(bf16[8,3584]{1,0:T(8,128)(2,1)} %param.6) | copy-start | bytes 172036
  105.3 26.4 %all-to-all-start.1 = ((bf16[16,6,3584]{2,1,0:T(8,128)(2,1)}), bf16[16,6,3584]{2,1,0:T(8,128)(2,1)S(1)}, u32[]{:S(2)}, u32[]{:S(2)}) async-start(bf16[16,6,3584]{2,1,0:T(8,128)(2,1)} %convert_element_type.103), calls=%async_computation.2 | async-start | bytes 1835008 | tf_op jit(solution)/shard_map/all_to_all | solution.py:70
  110.9 75.7 %all-gather.5.cloned.1.call-start = ((), (), s32[]{:S(2)}) async-start(), calls=%async_computation.8 | async-start | bytes 2064384 | tf_op jit(solution)/shard_map/all_gather | solution.py:61
  162.5 57.6 %reduce-scatter.5.cloned.1.call-start = ((), (), s32[]{:S(2)}) async-start(), calls=%async_computation.9 | async-start | bytes 2064384 | tf_op jit(solution)/shard_map/reduce_scatter | solution.py:67
  186.6 3.4 %copy-start.2 = (bf16[192,3584]{1,0:T(8,128)(2,1)S(1)}, bf16[192,3584]{1,0:T(8,128)(2,1)}, u32[]{:S(2)}) copy-start(bf16[192,3584]{1,0:T(8,128)(2,1)} %all-gather.5.cloned.1.call-done) | copy-start | bytes 4128772
  222.3 34.3 %all-to-all-start.3 = ((bf16[16,6,3584]{2,1,0:T(8,128)(2,1)}), bf16[16,6,3584]{2,1,0:T(8,128)(2,1)S(1)}, u32[]{:S(2)}, u32[]{:S(2)}) async-start(bf16[16,6,3584]{2,1,0:T(8,128)(2,1)} %convert_element_type.114), calls=%async_computation.5 | async-start | bytes 1835008 | tf_op jit(solution)/shard_map/all_to_all | solution.py:70
Sparse Core Ops, SparseCore 0:
  44.7 24.8 all-gather.2
  79.1 23.9 reduce-scatter.2
  162.7 23.8 all-gather.4
  196.1 23.9 reduce-scatter.4
